TPU v7x, 32 devices: a whole 2x2x4 slice. The times are simulated.
32 devices in a mesh: tile: 8 (over z, x), conv: 4 (over y, core).
Axes of the slice: x: 2, y: 2, z: 4, core: 2. Of those that a mesh axis runs over, the one named last changes fastest.
Arguments:
- field: float32 [256, 24576], P(None, ('tile', 'conv')), may hold values from -6 to 6
- interp: bfloat16 [32768, 384], P(('tile', 'conv')), may hold values from -0.1875 to 0.1875
- conv_blocks: bfloat16 [64, 3, 256, 256], P(('tile', 'conv')), may hold values from -0.21875 to 0.21875
- band_shift: int32 [64, 3], P(('tile', 'conv')), may hold values from 0 to 1
- owner: int32 [12288, 1], P(('tile', 'conv')), may hold values from 0 to 3; in each aligned block of 384 rows (0 to 383, 384 to 767, ...) at most 128 rows name the same one
- edge_index: int32 [64, 128], P(('tile', 'conv')), may hold values from 0 to 767, as said below
Outputs:
- correlated: float32 [256, 24576], P(None, ('tile', 'conv'))
Inputs may be any that keep to these rules, and one draw needn't show every extreme that they name: `edge_index`: row 2b lists the first 128 columns of domain b in some order, row 2b + 1 its last 128 columns in some order. Among the 384 points of one domain no owner is named more than 128 times, and in some domains one owner is named exactly 128 times.
All inputs are finite; a program needn't handle non-finite values.
Results may differ from a plain program's by a relative error of at most 0.0049.
Values may be sent and summed in bfloat16 or wider, within the bound.
A program may use at most 64 MiB of HBM per device.

v0:
```python
import jax
import jax.numpy as jnp
from jax import lax
from jax.sharding import PartitionSpec as P


def padded(cells, sides, width):
    for axis, dim in sides:
        count = lax.axis_size(axis)
        head = lax.slice_in_dim(cells, 0, width, axis=dim)
        tail = lax.slice_in_dim(cells, cells.shape[dim] - width, cells.shape[dim], axis=dim)
        cells = jnp.concatenate(
            [
                lax.ppermute(tail, axis, [(i, (i + 1) % count) for i in range(count)]),
                cells,
                lax.ppermute(head, axis, [((i + 1) % count, i) for i in range(count)]),
            ],
            axis=dim,
        )
    return cells


def contract_last(left_side, right_side):
    return lax.dot_general(
        left_side, right_side, (((1,), (1,)), ((), ())), preferred_element_type=jnp.float32
    )


def convolve(values, conv_blocks, band_shift):
    height = values.shape[0]
    owned_blocks = conv_blocks.shape[0]
    points = conv_blocks.shape[2]
    pieces = values.reshape(height, owned_blocks, points)
    source = (jnp.arange(owned_blocks, dtype=jnp.int32)[:, None] + band_shift) % owned_blocks
    select = (
        source[:, :, None] == jnp.arange(owned_blocks, dtype=jnp.int32)[None, None, :]
    ).astype(jnp.bfloat16)
    picked = jnp.einsum("rsp,jbs->rjbp", pieces, select, preferred_element_type=jnp.float32).astype(
        jnp.bfloat16
    )
    forward = jnp.einsum(
        "rjbp,jbpq->rjq", picked, conv_blocks, preferred_element_type=jnp.float32
    ).astype(jnp.bfloat16)
    backward = jnp.einsum(
        "rjq,jbpq->rjbp", forward, conv_blocks, preferred_element_type=jnp.float32
    )
    adjoint = jnp.einsum(
        "rjbp,jbs->rsp", backward, select.astype(jnp.float32), precision=lax.Precision.HIGHEST
    )
    return adjoint.reshape(height, owned_blocks * points).astype(jnp.bfloat16)


def on_device(field, interp, conv_blocks, band_shift, owner, edge_index):
    columns = field.shape[1]
    rim_width = edge_index.shape[1]
    groups = lax.axis_size("conv")
    slot_count = conv_blocks.shape[0] * conv_blocks.shape[2]
    capacity = slot_count // groups
    rounded = field.astype(jnp.bfloat16)
    left_list = edge_index[0]
    right_list = edge_index[1]
    rim_values = jnp.concatenate(
        [jnp.take(rounded, left_list, axis=1), jnp.take(rounded, right_list, axis=1)], axis=1
    )
    widened = padded(rim_values, ((("tile", "conv"), 1),), rim_width)
    from_left = widened[:, :rim_width]
    from_right = widened[:, 3 * rim_width :]
    extended = jnp.concatenate([from_left, rounded, from_right], axis=1)
    subgrid = jnp.dot(extended, interp, preferred_element_type=jnp.float32)
    subgrid = subgrid.astype(jnp.bfloat16)
    owners = owner[:, 0]
    choose = (owners[:, None] == jnp.arange(groups, dtype=jnp.int32)[None, :]).astype(jnp.int32)
    before = jnp.cumsum(choose, axis=0) - choose
    position = jnp.sum(before * choose, axis=1)
    slot_index = owners * capacity + position
    placement = (slot_index[:, None] == jnp.arange(slot_count, dtype=jnp.int32)[None, :]).astype(
        jnp.bfloat16
    )
    outgoing = jnp.dot(subgrid, placement, preferred_element_type=jnp.float32).astype(jnp.bfloat16)
    incoming = lax.all_to_all(
        convolve(
            lax.all_to_all(outgoing, "conv", split_axis=1, concat_axis=1, tiled=True),
            conv_blocks,
            band_shift,
        ),
        "conv",
        split_axis=1,
        concat_axis=1,
        tiled=True,
    )
    returned = contract_last(incoming, placement).astype(jnp.bfloat16)
    partial_value = contract_last(returned, interp)
    left_part = partial_value[:, :rim_width]
    right_part = partial_value[:, rim_width + columns :]
    edge_sums = padded(
        jnp.concatenate([left_part, right_part], axis=1).astype(jnp.bfloat16),
        ((("tile", "conv"), 1),),
        rim_width,
    ).astype(jnp.float32)
    interior_part = partial_value[:, rim_width : rim_width + columns]
    result = interior_part.at[:, left_list].add(edge_sums[:, :rim_width])
    result = result.at[:, right_list].add(edge_sums[:, 3 * rim_width :])
    return result


def solution(mesh):
    return jax.shard_map(
        on_device,
        mesh=mesh,
        in_specs=(
            P(None, ("tile", "conv")),
            P(("tile", "conv"), None),
            P(("tile", "conv"), None, None, None),
            P(("tile", "conv"), None),
            P(("tile", "conv"), None),
            P(("tile", "conv"), None),
        ),
        out_specs=P(None, ("tile", "conv")),
        check_vma=False,
    )
```

profile of v0, /device:TPU:0, one launch (start us, length us, event | category | flops | bytes accessed | tf_op | source)
XLA Modules:
  0.0 51.1 jit_solution(18035988229664410516)
XLA Ops:
  0.0 0.0 copy-start
  0.0 0.0 copy-start.1
  0.0 0.8 %compare_and_fusion.1 = (pred[128]{0:T(512)(128)(4,1)S(1)}, s32[128]{0:T(128)S(1)}, pred[128]{0:T(512)(128)(4,1)S(1)}, s32[128]{0:T(128)S(1)}) fusion(s32[2,128]{1,0:T(2,128)} %param.13), kind=kLoop, calls=%fused_computation.58 | loop fusion | flops 1536 | bytes 2304 | tf_op jit(solution)/shard_map/jit(_take)/and | solution.py:63
  0.8 1.3 %copy.27 = bf16[256,768]{0,1:T(8,128)(2,1)S(1)} copy(f32[256,768]{1,0:T(8,128)} %param.8) | data formatting | bytes 1179648 | tf_op args[0]
  2.1 0.8 %gather_fusion = bf16[128,256]{1,0:T(8,128)(2,1)S(1)} fusion(bf16[256,768]{0,1:T(8,128)(2,1)S(1)} %copy.27, s32[1024]{0:T(1024)S(1)} %pad_clamp_fusion.1), kind=kCustom, calls=%fused_computation.clone | custom fusion | bytes 131584 | tf_op jit(solution)/shard_map/jit(_take)/gather | solution.py:63
  3.0 0.1 select_bitcast_fusion.1
  3.1 0.5 %collective-permute-start = (bf16[256,128]{0,1:T(8,128)(2,1)S(1)}, bf16[256,128]{0,1:T(8,128)(2,1)S(1)}, u32[]{:S(2)}, u32[]{:S(2)}) collective-permute-start(bf16[256,128]{0,1:T(8,128)(2,1)S(1)} %select_bitcast_fusion.1), channel_id=1, source_target_pairs={{0,1},{1,2},{2,3},{3,4},{4,5},{5,6},{6,7},{7,8},{8,9},{9,10},{10,1... | collective-permute-start | bytes 196616 | tf_op jit(solution)/shard_map/ppermute | solution.py:14
  3.6 0.8 %gather_fusion.1 = bf16[128,256]{1,0:T(8,128)(2,1)S(1)} fusion(bf16[256,768]{0,1:T(8,128)(2,1)S(1)} %copy.27, s32[1024]{0:T(1024)S(1)} %pad_clamp_fusion), kind=kCustom, calls=%fused_computation.1.clone | custom fusion | bytes 131584 | tf_op jit(solution)/shard_map/jit(_take)/gather | solution.py:63
  4.5 0.1 select_bitcast_fusion
  4.5 6.0 %collective-permute-start.1 = (bf16[256,128]{0,1:T(8,128)(2,1)S(1)}, bf16[256,128]{0,1:T(8,128)(2,1)S(1)}, u32[]{:S(2)}, u32[]{:S(2)}) collective-permute-start(bf16[256,128]{0,1:T(8,128)(2,1)S(1)} %select_bitcast_fusion), channel_id=1, source_target_pairs={{1,0},{2,1},{3,2},{4,3},{5,4},{6,5},{7,6},{8,7},{9,8},{10,9},{11,1... | collective-permute-start | bytes 196616 | tf_op jit(solution)/shard_map/ppermute | solution.py:16
  10.5 0.0 copy-done.1
  10.6 1.2 %reduce-window.6 = s32[4,3,128]{2,1,0:T(4,128)S(1)} reduce-window(s32[4,3,128]{2,1,0:T(4,128)S(1)} %fusion.32, s32[]{:T(128)} %constant.30.clone.1), window={size=1x1x128 pad=0_0x0_0x127_0}, to_apply=%region_0.0 | reduce-window | flops 195072 | bytes 12292 | tf_op jit(solution)/shard_map/reduce-window
  11.8 0.2 slice_reduce_fusion
  12.0 0.2 reduce-window.9
  12.2 0.1 add_bitcast_fusion
  12.3 0.0 copy-start.3
  12.3 0.0 collective-permute-done
  12.3 0.1 collective-permute-done.1
  12.4 0.0 copy-done
  12.4 0.7 %fusion.10 = bf16[32,4,8,128]{3,2,1,0:T(8,128)(2,1)S(1)} fusion(bf16[1024,384]{1,0:T(8,128)(2,1)S(1)} %copy-done, bf16[256,128]{0,1:T(8,128)(2,1)S(1)} %collective-permute-done.1, bf16[256,768]{0,1:T(8,128)(2,1)S(1)} %copy.27, bf16[256,128]{0,1:T(8,128)(2,1)S(1)} %collective-permute-done, s32[384]{0:T(512)S(1)} %add_reduce_fusion), kind=kOutput, calls=%fused_computation.16 | convolution fusion | flops 303988736 | bytes 1574400 | tf_op jit(solution)/shard_map/dot_general | solution.py:79
  13.1 0.7 %copy.58 = bf16[32,4,8,128]{3,2,0,1:T(8,128)(2,1)} copy(bf16[32,4,8,128]{3,2,1,0:T(8,128)(2,1)S(1)} %fusion.10) | data formatting | bytes 524288 | tf_op jit(solution)/shard_map/all_to_all | solution.py:82
  13.9 3.4 %all-to-all-start = ((bf16[256,4,128]{2,0,1:T(8,128)(2,1)}), bf16[256,4,128]{2,0,1:T(8,128)(2,1)S(1)}, u32[]{:S(2)}, u32[]{:S(2)}) async-start(bf16[256,4,128]{2,0,1:T(8,128)(2,1)} %bitcast.89), calls=%async_computation | async-start | bytes 524288 | tf_op jit(solution)/shard_map/all_to_all | solution.py:82
  17.3 0.0 copy-done.3
  17.3 5.9 %all-to-all-done = bf16[256,4,128]{2,0,1:T(8,128)(2,1)S(1)} async-done(((bf16[256,4,128]{2,0,1:T(8,128)(2,1)}), bf16[256,4,128]{2,0,1:T(8,128)(2,1)S(1)}, u32[]{:S(2)}, u32[]{:S(2)}) %all-to-all-start) | async-done | bytes 262176 | tf_op jit(solution)/shard_map/all_to_all | solution.py:82
  23.3 0.2 copy.29
  23.5 0.2 reshape.131
  23.7 1.0 %fusion.2 = bf16[256,2,3,256]{3,2,0,1:T(4,128)(2,1)S(1)} fusion(bf16[256,2,256,1]{2,1,0,3:T(2,128)(2,1)S(1)} %reshape.131, s32[2,3]{1,0:T(2,128)S(1)} %and_select_fusion), kind=kOutput, calls=%fused_computation.8 | convolution fusion | flops 1966092 | bytes 1048600 | tf_op jit(solution)/shard_map/rsp,jbs->rjbp/dot_general | solution.py:38
  24.7 2.0 %convolution_bitcast_fusion = f32[256,2,3,256]{3,0,2,1:T(8,128)S(1)} fusion(bf16[2,3,256,256]{3,2,1,0:T(8,128)(2,1)} %param.10, bf16[256,2,3,256]{3,2,0,1:T(4,128)(2,1)S(1)} %fusion.2), kind=kOutput, calls=%fused_computation.6 | convolution fusion | flops 402784256 | bytes 3145728 | tf_op jit(solution)/shard_map/rjq,jbpq->rjbp/dot_general | solution.py:44
  26.7 2.9 %fusion.11 = bf16[256,2,256]{2,1,0:T(2,128)(2,1)S(1)} fusion(f32[256,2,3,256]{3,0,2,1:T(8,128)S(1)} %convolution_bitcast_fusion, s32[2,3]{1,0:T(2,128)S(1)} %and_select_fusion), kind=kOutput, calls=%fused_computation.17 | convolution fusion | flops 9568268 | bytes 1835032 | tf_op jit(solution)/shard_map/rjbp,jbs->rsp/dot_general | solution.py:47
  29.6 0.2 convert_element_type.59
  29.9 8.4 %all_to_all.18 = bf16[256,4,128]{2,0,1:T(8,128)(2,1)S(1)} all-to-all(bf16[256,4,128]{2,0,1:T(8,128)(2,1)S(1)} %copy.32), channel_id=1, replica_groups=mesh['tile'=8,'conv'=4] {'conv'}, dimensions={1} | all-to-all | bytes 524288 | tf_op jit(solution)/shard_map/all_to_all | solution.py:80
  38.3 0.1 copy.33
  38.4 0.0 copy-start.2
  38.4 0.8 %fusion.46 = (bf16[256,1024]{1,0:T(8,128)(2,1)S(1)}, f32[256,1024]{1,0:T(8,128)S(1)}) fusion(bf16[1024,384]{1,0:T(8,128)(2,1)S(1)} %copy-done, bf16[256,512]{0,1:T(8,128)(2,1)S(1)} %bitcast.91, s32[384]{0:T(512)S(1)} %add_reduce_fusion), kind=kOutput, calls=%fused_computation.68 | convolution fusion | flops 302546944 | bytes 2622976 | tf_op jit(solution)/shard_map/dot_general | solution.py:24
  39.2 0.1 collective-permute-start.2
  39.3 5.3 %collective-permute-start.3 = (bf16[256,128]{1,0:T(8,128)(2,1)S(1)}, bf16[256,128]{1,0:T(8,128)(2,1)S(1)}, u32[]{:S(2)}, u32[]{:S(2)}) collective-permute-start(bf16[256,128]{1,0:T(8,128)(2,1)S(1)} %get-tuple-element.11), channel_id=1, source_target_pairs={{1,0},{2,1},{3,2},{4,3},{5,4},{6,5},{7,6},{8,7},{9,8},{10,9},{11,1... | collective-permute-start | bytes 196616 | tf_op jit(solution)/shard_map/ppermute | solution.py:16
  44.6 0.0 copy-done.2
  44.6 0.1 slice.45
  44.7 0.3 copy.34
  45.0 1.6 %collective-permute-done.2 = bf16[256,128]{1,0:T(8,128)(2,1)S(1)} collective-permute-done((bf16[256,128]{1,0:T(8,128)(2,1)S(1)}, bf16[256,128]{1,0:T(8,128)(2,1)S(1)}, u32[]{:S(2)}, u32[]{:S(2)}) %collective-permute-start.2) | collective-permute-done | bytes 65568 | tf_op jit(solution)/shard_map/ppermute | solution.py:14
  46.6 0.0 collective-permute-done.3
  46.6 0.1 copy.35
  46.7 0.1 copy.36
  46.8 1.6 %scatter_fusion = f32[256,768]{0,1:T(8,128)S(1)} fusion(f32[256,768]{0,1:T(8,128)S(1)} %copy.34, s32[128]{0:T(128)S(1)} %get-tuple-element.15, f32[128,256]{1,0:T(8,128)S(1)} %copy.35), kind=kCustom, calls=%fused_computation.2 | custom fusion | flops 32768 | bytes 393728 | tf_op jit(solution)/shard_map/scatter-add | solution.py:101
  48.4 1.6 %scatter_fusion.1 = f32[256,768]{0,1:T(8,128)S(1)} fusion(f32[256,768]{0,1:T(8,128)S(1)} %scatter_fusion, s32[128]{0:T(128)S(1)} %get-tuple-element.14, f32[128,256]{1,0:T(8,128)S(1)} %copy.36), kind=kCustom, calls=%fused_computation.3 | custom fusion | flops 32768 | bytes 393728 | tf_op jit(solution)/shard_map/scatter-add | solution.py:102
  50.0 1.1 %copy.37 = f32[256,768]{1,0:T(8,128)} copy(f32[256,768]{0,1:T(8,128)S(1)} %scatter_fusion.1) | data formatting | bytes 1572864 | tf_op jit(solution)/shard_map/scatter-add | solution.py:102
  (11 shorter events, 0.2 us)
Async XLA Ops:
  0.0 12.4 %copy-start = (bf16[1024,384]{1,0:T(8,128)(2,1)S(1)}, bf16[1024,384]{1,0:T(8,128)(2,1)}, u32[]{:S(2)}) copy-start(bf16[1024,384]{1,0:T(8,128)(2,1)} %param.9) | copy-start | bytes 2359300
  0.0 10.5 %copy-start.1 = (s32[384,1]{0,1:T(1,128)S(1)}, s32[384,1]{0,1:T(1,128)}, u32[]{:S(2)}) copy-start(s32[384,1]{0,1:T(1,128)} %param.12) | copy-start | bytes 4612
  3.1 9.3 %collective-permute-start = (bf16[256,128]{0,1:T(8,128)(2,1)S(1)}, bf16[256,128]{0,1:T(8,128)(2,1)S(1)}, u32[]{:S(2)}, u32[]{:S(2)}) collective-permute-start(bf16[256,128]{0,1:T(8,128)(2,1)S(1)} %select_bitcast_fusion.1), channel_id=1, source_target_pairs={{0,1},{1,2},{2,3},{3,4},{4,5},{5,6},{6,7},{7,8},{8,9},{9,10},{10,1... | collective-permute-start | bytes 196616 | tf_op jit(solution)/shard_map/ppermute | solution.py:14
  4.5 7.9 %collective-permute-start.1 = (bf16[256,128]{0,1:T(8,128)(2,1)S(1)}, bf16[256,128]{0,1:T(8,128)(2,1)S(1)}, u32[]{:S(2)}, u32[]{:S(2)}) collective-permute-start(bf16[256,128]{0,1:T(8,128)(2,1)S(1)} %select_bitcast_fusion), channel_id=1, source_target_pairs={{1,0},{2,1},{3,2},{4,3},{5,4},{6,5},{7,6},{8,7},{9,8},{10,9},{11,1... | collective-permute-start | bytes 196616 | tf_op jit(solution)/shard_map/ppermute | solution.py:16
  12.3 5.0 %copy-start.3 = (s32[2,3]{1,0:T(2,128)S(1)}, s32[2,3]{1,0:T(2,128)}, u32[]{:S(2)}) copy-start(s32[2,3]{1,0:T(2,128)} %param.11) | copy-start | bytes 76
  13.9 9.4 %all-to-all-start = ((bf16[256,4,128]{2,0,1:T(8,128)(2,1)}), bf16[256,4,128]{2,0,1:T(8,128)(2,1)S(1)}, u32[]{:S(2)}, u32[]{:S(2)}) async-start(bf16[256,4,128]{2,0,1:T(8,128)(2,1)} %bitcast.89), calls=%async_computation | async-start | bytes 524288 | tf_op jit(solution)/shard_map/all_to_all | solution.py:82
  38.4 6.2 %copy-start.2 = (s32[2,128]{1,0:T(2,128)S(1)}, s32[2,128]{1,0:T(2,128)}, u32[]{:S(2)}) copy-start(s32[2,128]{1,0:T(2,128)} %param.13) | copy-start | bytes 3076
  39.2 7.3 %collective-permute-start.2 = (bf16[256,128]{1,0:T(8,128)(2,1)S(1)}, bf16[256,128]{1,0:T(8,128)(2,1)S(1)}, u32[]{:S(2)}, u32[]{:S(2)}) collective-permute-start(bf16[256,128]{1,0:T(8,128)(2,1)S(1)} %get-tuple-element.10), channel_id=1, source_target_pairs={{0,1},{1,2},{2,3},{3,4},{4,5},{5,6},{6,7},{7,8},{8,9},{9,10},{10,1... | collective-permute-start | bytes 196616 | tf_op jit(solution)/shard_map/ppermute | solution.py:14
  39.3 7.3 %collective-permute-start.3 = (bf16[256,128]{1,0:T(8,128)(2,1)S(1)}, bf16[256,128]{1,0:T(8,128)(2,1)S(1)}, u32[]{:S(2)}, u32[]{:S(2)}) collective-permute-start(bf16[256,128]{1,0:T(8,128)(2,1)S(1)} %get-tuple-element.11), channel_id=1, source_target_pairs={{1,0},{2,1},{3,2},{4,3},{5,4},{6,5},{7,6},{8,7},{9,8},{10,9},{11,1... | collective-permute-start | bytes 196616 | tf_op jit(solution)/shard_map/ppermute | solution.py:16
where the time goes:
time: 51.4 us; the launch traced here: 51.1 us
  starting transfers between devices  15.3 us (30%)
  blocking collectives  8.39 us (16%)
  waiting for transfers between devices  7.66 us (15%)
  matrix products  7.43 us (14%)
  local copies, waits for them, and re-layouts  6.38 us (12%)
  other arithmetic  5.73 us (11%)
    ppermute x2, starting transfers between devices, padded(): lax.ppermute(head, axis, [((i + 1) % count, i) for i in range(count)])  11.3 us
    all_to_all x1, blocking collectives, on_device(): lax.all_to_all(convolve(lax.all_to_all(outgoing, 'conv', split_axis=1, co...  8.39 us
    all_to_all x1, waiting for transfers between devices, on_device(): lax.all_to_all(outgoing, 'conv', split_axis=1, concat_axis=1, tiled=True)  5.95 us
    all_to_all x1, starting transfers between devices, on_device(): lax.all_to_all(outgoing, 'conv', split_axis=1, concat_axis=1, tiled=True)  3.41 us
    dot_general x1, matrix products, convolve(): jnp.einsum('rjbp,jbs->rsp', backward, select.astype(jnp.float32), precisi...  2.94 us
    dot_general x1, matrix products, convolve(): jnp.einsum('rjq,jbpq->rjbp', forward, conv_blocks, preferred_element_type...  2.02 us
    ppermute x2, waiting for transfers between devices, padded(): lax.ppermute(tail, axis, [(i, (i + 1) % count) for i in range(count)])  1.61 us
    scatter-add x1, other arithmetic, on_device(): result = result.at[:, right_list].add(edge_sums[:, 3 * rim_width:])  1.59 us
  transfers between devices with their start and end apart: 5, of which 3 were waited for; matrix products, arithmetic and copies ran while one was open for 6% of the time, Pallas kernels for 0%

commit v1 on v0

v1 whole, which is shorter than its diff:
```python
import functools

import jax
import jax.numpy as jnp
from jax import lax
from jax.experimental import pallas as pl
from jax.experimental.pallas import tpu as pltpu
from jax.sharding import PartitionSpec as P

MESH = pl.DeviceIdType.MESH
CHUNKS = 1


def mm(left, right):
    return lax.dot_general(left, right, (((1,), (0,)), ((), ())), preferred_element_type=jnp.float32)


def mm_t(left, right):
    return lax.dot_general(left, right, (((1,), (1,)), ((), ())), preferred_element_type=jnp.float32)


def kernel(
    tiles, groups, field_hbm, interp_hbm, blocks_hbm, shift_ref, owner_hbm, edge_hbm, out_hbm,
    field, interp, blocks, owner, edge, ip, conv, gram, base, result,
    edge_out, edge_in, slot_out, slot_in, back_out, back_in, part_out, part_in,
    load_sem, store_sem, edge_send, edge_recv, slot_send, slot_recv, back_send, back_recv,
    part_send, part_recv,
):
    rows, columns = field.shape
    extended, points = interp.shape
    rim = edge.shape[1]
    owned, bands, size = blocks.shape[0], blocks.shape[1], blocks.shape[2]
    slots = owned * size
    capacity = slots // groups
    height = rows // CHUNKS
    tile, me = lax.axis_index("tile"), lax.axis_index("conv")
    count = tiles * groups
    place = tile * groups + me
    after, before = lax.rem(place + 1, count), lax.rem(place + count - 1, count)
    right = (lax.div(after, groups), lax.rem(after, groups))
    left = (lax.div(before, groups), lax.rem(before, groups))
    hops = [groups // 2] + [k for k in range(1, groups) if k != groups // 2]
    peers = [lax.rem(me + k, groups) for k in hops]

    barrier = pltpu.get_barrier_semaphore()
    for other in [left, right] + [(tile, peer) for peer in peers]:
        pl.semaphore_signal(barrier, inc=1, device_id=other, device_id_type=MESH)

    def load(source, target, index):
        copy = pltpu.make_async_copy(source, target, load_sem.at[index])
        copy.start()
        return copy

    inner = slice(rim, columns - rim)
    lead, tail = slice(0, rim), slice(columns - rim, columns)
    load_edge = load(edge_hbm, edge, 0)
    load_lead = load(field_hbm.at[:, lead], field.at[:, lead], 1)
    load_tail = load(field_hbm.at[:, tail], field.at[:, tail], 2)
    load_owner = load(owner_hbm, owner, 3)
    load_interp = load(interp_hbm, interp, 4)
    load_inner = load(field_hbm.at[:, inner], field.at[:, inner], 5)
    load_blocks = load(blocks_hbm, blocks, 6)

    def piece(chunk):
        return slice(chunk * height, (chunk + 1) * height)

    def pair(send, recv, out_ref, in_ref, chunk, side, target):
        return pltpu.make_async_remote_copy(
            src_ref=out_ref.at[chunk, side], dst_ref=in_ref.at[chunk, side],
            send_sem=send.at[chunk, side], recv_sem=recv.at[chunk, side],
            device_id=target, device_id_type=MESH,
        )

    def exchange(send, recv, out_ref, in_ref, chunk):
        copies = []
        for peer in peers:
            copies.append(pltpu.make_async_remote_copy(
                src_ref=out_ref.at[chunk, peer], dst_ref=in_ref.at[chunk, me],
                send_sem=send.at[chunk, peer], recv_sem=recv.at[chunk, me],
                device_id=(tile, peer), device_id_type=MESH,
            ))
            copies[-1].start()
        in_ref[chunk, me] = out_ref[chunk, me]
        return copies

    def arrived(send, recv, out_ref, in_ref, chunk):
        for peer in peers:
            pltpu.make_async_remote_copy(
                src_ref=out_ref.at[chunk, peer], dst_ref=in_ref.at[chunk, peer],
                send_sem=send.at[chunk, peer], recv_sem=recv.at[chunk, peer],
                device_id=(tile, peer), device_id_type=MESH,
            ).wait_recv()
        return jnp.concatenate([in_ref[chunk, g] for g in range(groups)], axis=1)

    load_edge.wait()
    lines = lax.broadcasted_iota(jnp.int32, (rim, rim), 0)
    left_pick = (lines == edge[0:1, :]).astype(jnp.float32).astype(jnp.bfloat16)
    right_pick = (lines + (columns - rim) == edge[1:2, :]).astype(jnp.float32).astype(jnp.bfloat16)
    load_lead.wait()
    load_tail.wait()
    for chunk in range(CHUNKS):
        part = piece(chunk)
        edge_out[chunk, 0] = mm(field[part, tail].astype(jnp.bfloat16), right_pick).astype(jnp.bfloat16)
        edge_out[chunk, 1] = mm(field[part, lead].astype(jnp.bfloat16), left_pick).astype(jnp.bfloat16)
    pl.semaphore_wait(barrier, 2 + len(peers))
    edge_copies, part_copies, slot_copies, back_copies = [], [], [], []
    for chunk in range(CHUNKS):
        for side, target in ((0, right), (1, left)):
            copy = pair(edge_send, edge_recv, edge_out, edge_in, chunk, side, target)
            copy.start()
            edge_copies.append(copy)

    load_owner.wait()
    owners = owner[...]
    choose = (owners == lax.broadcasted_iota(jnp.int32, (-(-groups // 8) * 8, points), 0)).astype(jnp.float32)
    order = lax.broadcasted_iota(jnp.int32, (points, points), 0) < lax.broadcasted_iota(
        jnp.int32, (points, points), 1
    )
    ranks = mm(choose.astype(jnp.bfloat16), order.astype(jnp.float32).astype(jnp.bfloat16))
    rank = jnp.sum(ranks * choose, axis=0, keepdims=True)
    slot = owners * capacity + rank.astype(jnp.int32)
    placement = (slot == lax.broadcasted_iota(jnp.int32, (slots, points), 0)).astype(jnp.float32)
    placement = placement.astype(jnp.bfloat16)
    load_interp.wait()
    ip[0:rim, :] = mm_t(interp[0:rim, :], placement).astype(jnp.bfloat16)
    ip[rim : 2 * rim, :] = mm_t(interp[extended - rim :, :], placement).astype(jnp.bfloat16)
    ip[2 * rim :, :] = mm_t(interp[rim : extended - rim, :], placement).astype(jnp.bfloat16)
    load_inner.wait()
    base[...] = mm(field[...].astype(jnp.bfloat16), ip[2 * rim :, :])

    load_blocks.wait()
    for j in range(owned):
        for s in range(owned):
            total = jnp.zeros((size, size), jnp.float32)
            for c in range(bands):
                reads = lax.rem(j + shift_ref[j, c], owned) == s
                total = total + jnp.where(reads, 1.0, 0.0) * blocks[j, c].astype(jnp.float32)
            conv[s * size : (s + 1) * size, j * size : (j + 1) * size] = total.astype(jnp.bfloat16)
    gram[...] = mm_t(conv[...], conv[...]).astype(jnp.bfloat16)

    for chunk in range(CHUNKS):
        for side, target in ((0, right), (1, left)):
            pair(edge_send, edge_recv, edge_out, edge_in, chunk, side, target).wait_recv()
        edges = jnp.concatenate([edge_in[chunk, 0], edge_in[chunk, 1]], axis=1)
        subgrid = (base[piece(chunk), :] + mm(edges, ip[0 : 2 * rim, :])).astype(jnp.bfloat16)
        for g in range(groups):
            slot_out[chunk, g] = subgrid[:, g * capacity : (g + 1) * capacity]
        slot_copies += exchange(slot_send, slot_recv, slot_out, slot_in, chunk)

    for chunk in range(CHUNKS):
        gathered = arrived(slot_send, slot_recv, slot_out, slot_in, chunk)
        adjoint = mm(gathered, gram[...]).astype(jnp.bfloat16)
        for g in range(groups):
            back_out[chunk, g] = adjoint[:, g * capacity : (g + 1) * capacity]
        back_copies += exchange(back_send, back_recv, back_out, back_in, chunk)

    stores = []
    for chunk in range(CHUNKS):
        part = piece(chunk)
        returned = arrived(back_send, back_recv, back_out, back_in, chunk)
        rims = mm_t(returned, ip[0 : 2 * rim, :]).astype(jnp.bfloat16)
        part_out[chunk, 0] = rims[:, rim:]
        part_out[chunk, 1] = rims[:, :rim]
        for side, target in ((0, right), (1, left)):
            copy = pair(part_send, part_recv, part_out, part_in, chunk, side, target)
            copy.start()
            part_copies.append(copy)
        result[part, :] = mm_t(returned, ip[2 * rim :, :])
        copy = pltpu.make_async_copy(
            result.at[part, inner], out_hbm.at[part, inner], store_sem.at[chunk, 0]
        )
        copy.start()
        stores.append(copy)

    for chunk in range(CHUNKS):
        part = piece(chunk)
        for side, where, pick, target in ((0, lead, left_pick, right), (1, tail, right_pick, left)):
            pair(part_send, part_recv, part_out, part_in, chunk, side, target).wait_recv()
            result[part, where] += mm_t(part_in[chunk, side], pick)
            copy = pltpu.make_async_copy(
                result.at[part, where], out_hbm.at[part, where], store_sem.at[chunk, 1 + side]
            )
            copy.start()
            stores.append(copy)
    for copy in edge_copies + slot_copies + back_copies + part_copies:
        copy.wait_send()
    for copy in stores:
        copy.wait()


def on_device(tiles, groups, field, interp, conv_blocks, band_shift, owner, edge_index):
    rows, columns = field.shape
    extended, points = interp.shape
    rim = edge_index.shape[1]
    slots = conv_blocks.shape[0] * conv_blocks.shape[2]
    capacity = slots // groups
    height = rows // CHUNKS
    half, single = jnp.bfloat16, jnp.float32
    sides = pltpu.VMEM((CHUNKS, 2, height, rim), half)
    cells = pltpu.VMEM((CHUNKS, groups, height, capacity), half)
    two, many = pltpu.SemaphoreType.DMA((CHUNKS, 2)), pltpu.SemaphoreType.DMA((CHUNKS, groups))
    anywhere = pl.BlockSpec(memory_space=pl.ANY)
    return pl.pallas_call(
        functools.partial(kernel, tiles, groups),
        out_shape=jax.ShapeDtypeStruct(field.shape, single),
        in_specs=[anywhere] * 3 + [pl.BlockSpec(memory_space=pltpu.SMEM)] + [anywhere] * 2,
        out_specs=anywhere,
        scratch_shapes=[
            pltpu.VMEM(field.shape, single),
            pltpu.VMEM(interp.shape, half),
            pltpu.VMEM(conv_blocks.shape, half),
            pltpu.VMEM((1, points), jnp.int32),
            pltpu.VMEM(edge_index.shape, jnp.int32),
            pltpu.VMEM((extended, slots), half),
            pltpu.VMEM((slots, slots), half),
            pltpu.VMEM((slots, slots), half),
            pltpu.VMEM((rows, slots), single),
            pltpu.VMEM(field.shape, single),
            sides, sides, cells, cells, cells, cells, sides, sides,
            pltpu.SemaphoreType.DMA((7,)),
            pltpu.SemaphoreType.DMA((CHUNKS, 3)),
            two, two, many, many, many, many, two, two,
        ],
        compiler_params=pltpu.CompilerParams(collective_id=0, has_side_effects=True),
    )(field, interp, conv_blocks, band_shift, owner.reshape(1, points), edge_index)


def solution(mesh):
    return jax.shard_map(
        functools.partial(on_device, mesh.shape["tile"], mesh.shape["conv"]),
        mesh=mesh,
        in_specs=(
            P(None, ("tile", "conv")),
            P(("tile", "conv"), None),
            P(("tile", "conv"), None, None, None),
            P(("tile", "conv"), None),
            P(("tile", "conv"), None),
            P(("tile", "conv"), None),
        ),
        out_specs=P(None, ("tile", "conv")),
        check_vma=False,
    )
```

time: 51.4 us -> 27.9 us (0.54)
  Pallas kernels: 0 us -> 25.6 us
  starting transfers between devices: 15.3 us -> 0 us
  blocking collectives: 8.39 us -> 0 us
  waiting for transfers between devices: 7.66 us -> 0 us
  matrix products: 7.43 us -> 0 us
  other arithmetic: 5.73 us -> 0 us
  local copies, waits for them, and re-layouts: 6.38 us -> 2.06 us
    pallas_call x0 -> x1, Pallas kernels: none -> 25.6 us  [on_device(): pl.pallas_call(functools.partial(kernel, tiles, groups), out_shape=jax.Sh...]
    ppermute x4 -> x0, starting transfers between devices: 11.9 us -> none  [the longest x2 11.3 us: padded(): lax.ppermute(head, axis, [((i + 1) % count, i) for i in range(count)])]
    all_to_all x1 -> x0, blocking collectives: 8.39 us -> none  [on_device(): lax.all_to_all(convolve(lax.all_to_all(outgoing, 'conv', split_axis=1, co...]
    dot_general x5 -> x0, matrix products: 7.43 us -> none  [the longest x1 2.94 us: convolve(): jnp.einsum('rjbp,jbs->rsp', backward, select.astype(jnp.float32), precisi...]
    all_to_all x1 -> x0, waiting for transfers between devices: 5.95 us -> none  [on_device(): lax.all_to_all(outgoing, 'conv', split_axis=1, concat_axis=1, tiled=True)]
    all_to_all x1 -> x0, starting transfers between devices: 3.41 us -> none  [on_device(): lax.all_to_all(outgoing, 'conv', split_axis=1, concat_axis=1, tiled=True)]
    scatter-add x2 -> x0, other arithmetic: 3.17 us -> none  [the longest x1 1.59 us: on_device(): result = result.at[:, right_list].add(edge_sums[:, 3 * rim_width:])]
    ppermute x4 -> x0, waiting for transfers between devices: 1.71 us -> none  [the longest x2 1.61 us: padded(): lax.ppermute(tail, axis, [(i, (i + 1) % count) for i in range(count)])]
  transfers between devices with their start and end apart: 5 -> 0, of which waited for: 3 -> 0; matrix products, arithmetic and copies ran while one was open for 6% -> 0% of each run, Pallas kernels for 0% -> 0%
where the time goes in v1:
time: 27.9 us; the launch traced here: 27.7 us
  Pallas kernels  25.6 us (92%)
  local copies, waits for them, and re-layouts  2.06 us (7%)
    pallas_call x1, Pallas kernels, on_device(): pl.pallas_call(functools.partial(kernel, tiles, groups), out_shape=jax.Sh...  25.6 us
    unnamed x1, local copies, waits for them, and re-layouts  2.06 us

profile of v1, /device:TPU:0, one launch (start us, length us, event | category | flops | bytes accessed | tf_op | source)
XLA Modules:
  0.0 27.7 jit_solution(14340509695640172974)
XLA Ops:
  0.0 25.6 %shard_map.64 = f32[256,768]{1,0:T(8,128)} custom-call(f32[256,768]{1,0:T(8,128)} %field_hbm.1, bf16[1024,384]{1,0:T(8,128)(2,1)} %interp_hbm.1, bf16[2,3,256,256]{3,2,1,0:T(8,128)(2,1)} %blocks_hbm.1, s32[2,3]{1,0:T(2,128)} %shift_ref.1, s32[1,384]{1,0:T(1,128)} %bitcast.1, s32[2,128]{1,0:T(2,128)} %edge_hbm.1), custom_call_target="tpu_custom_call" | custom-call | tf_op jit(solution)/shard_map/pallas_call | solution.py:203
  25.6 2.1 %copy.8 = f32[256,768]{1,0:T(8,128)} copy(f32[256,768]{1,0:T(8,128)} %shard_map.64) | data formatting | bytes 1572864

commit v2 on v1

--- a/solution.py
+++ b/solution.py
@@ -8,7 +8,7 @@
 from jax.sharding import PartitionSpec as P
 
 MESH = pl.DeviceIdType.MESH
-CHUNKS = 1
+CHUNKS = 2
 
 
 def mm(left, right):

time: 27.9 us -> 27.1 us (0.971)
  Pallas kernels: 25.6 us -> 24.9 us
    pallas_call x1, Pallas kernels: 25.6 us -> 24.9 us  [on_device(): pl.pallas_call(functools.partial(kernel, tiles, groups), out_shape=jax.Sh...]
where the time goes in v2:
time: 27.1 us; the launch traced here: 26.9 us
  Pallas kernels  24.9 us (92%)
  local copies, waits for them, and re-layouts  2.06 us (8%)
    pallas_call x1, Pallas kernels, on_device(): pl.pallas_call(functools.partial(kernel, tiles, groups), out_shape=jax.Sh...  24.9 us
    unnamed x1, local copies, waits for them, and re-layouts  2.06 us

profile of v2, /device:TPU:0, one launch (start us, length us, event | category | flops | bytes accessed | tf_op | source)
XLA Modules:
  0.0 26.9 jit_solution(8514711599912971456)
XLA Ops:
  0.0 24.9 %shard_map.64 = f32[256,768]{1,0:T(8,128)} custom-call(f32[256,768]{1,0:T(8,128)} %field_hbm.1, bf16[1024,384]{1,0:T(8,128)(2,1)} %interp_hbm.1, bf16[2,3,256,256]{3,2,1,0:T(8,128)(2,1)} %blocks_hbm.1, s32[2,3]{1,0:T(2,128)} %shift_ref.1, s32[1,384]{1,0:T(1,128)} %bitcast.1, s32[2,128]{1,0:T(2,128)} %edge_hbm.1), custom_call_target="tpu_custom_call" | custom-call | tf_op jit(solution)/shard_map/pallas_call | solution.py:203
  24.9 2.1 %copy.8 = f32[256,768]{1,0:T(8,128)} copy(f32[256,768]{1,0:T(8,128)} %shard_map.64) | data formatting | bytes 1572864

commit v3 on v2

--- a/solution.py
+++ b/solution.py
@@ -20,15 +20,14 @@
 
 
 def kernel(
-    tiles, groups, field_hbm, interp_hbm, blocks_hbm, shift_ref, owner_hbm, edge_hbm, out_hbm,
-    field, interp, blocks, owner, edge, ip, conv, gram, base, result,
+    tiles, groups, rim, field_hbm, interp_hbm, blocks_hbm, lists, result,
+    field, interp, blocks, ip, conv, gram, base,
     edge_out, edge_in, slot_out, slot_in, back_out, back_in, part_out, part_in,
-    load_sem, store_sem, edge_send, edge_recv, slot_send, slot_recv, back_send, back_recv,
+    load_sem, edge_send, edge_recv, slot_send, slot_recv, back_send, back_recv,
     part_send, part_recv,
 ):
     rows, columns = field.shape
     extended, points = interp.shape
-    rim = edge.shape[1]
     owned, bands, size = blocks.shape[0], blocks.shape[1], blocks.shape[2]
     slots = owned * size
     capacity = slots // groups
@@ -53,10 +52,8 @@
 
     inner = slice(rim, columns - rim)
     lead, tail = slice(0, rim), slice(columns - rim, columns)
-    load_edge = load(edge_hbm, edge, 0)
     load_lead = load(field_hbm.at[:, lead], field.at[:, lead], 1)
     load_tail = load(field_hbm.at[:, tail], field.at[:, tail], 2)
-    load_owner = load(owner_hbm, owner, 3)
     load_interp = load(interp_hbm, interp, 4)
     load_inner = load(field_hbm.at[:, inner], field.at[:, inner], 5)
     load_blocks = load(blocks_hbm, blocks, 6)
@@ -92,10 +89,11 @@
             ).wait_recv()
         return jnp.concatenate([in_ref[chunk, g] for g in range(groups)], axis=1)
 
-    load_edge.wait()
+    left_list = lists[:, points : points + rim]
+    right_list = lists[:, points + rim : points + 2 * rim]
     lines = lax.broadcasted_iota(jnp.int32, (rim, rim), 0)
-    left_pick = (lines == edge[0:1, :]).astype(jnp.float32).astype(jnp.bfloat16)
-    right_pick = (lines + (columns - rim) == edge[1:2, :]).astype(jnp.float32).astype(jnp.bfloat16)
+    left_pick = (lines == left_list).astype(jnp.float32).astype(jnp.bfloat16)
+    right_pick = (lines + (columns - rim) == right_list).astype(jnp.float32).astype(jnp.bfloat16)
     load_lead.wait()
     load_tail.wait()
     for chunk in range(CHUNKS):
@@ -110,8 +108,7 @@
             copy.start()
             edge_copies.append(copy)
 
-    load_owner.wait()
-    owners = owner[...]
+    owners = lists[:, 0:points]
     choose = (owners == lax.broadcasted_iota(jnp.int32, (-(-groups // 8) * 8, points), 0)).astype(jnp.float32)
     order = lax.broadcasted_iota(jnp.int32, (points, points), 0) < lax.broadcasted_iota(
         jnp.int32, (points, points), 1
@@ -133,7 +130,8 @@
         for s in range(owned):
             total = jnp.zeros((size, size), jnp.float32)
             for c in range(bands):
-                reads = lax.rem(j + shift_ref[j, c], owned) == s
+                at = points + 2 * rim + j * bands + c
+                reads = lax.rem(j + lists[:, at : at + 1], owned) == s
                 total = total + jnp.where(reads, 1.0, 0.0) * blocks[j, c].astype(jnp.float32)
             conv[s * size : (s + 1) * size, j * size : (j + 1) * size] = total.astype(jnp.bfloat16)
     gram[...] = mm_t(conv[...], conv[...]).astype(jnp.bfloat16)
@@ -154,7 +152,6 @@
             back_out[chunk, g] = adjoint[:, g * capacity : (g + 1) * capacity]
         back_copies += exchange(back_send, back_recv, back_out, back_in, chunk)
 
-    stores = []
     for chunk in range(CHUNKS):
         part = piece(chunk)
         returned = arrived(back_send, back_recv, back_out, back_in, chunk)
@@ -166,26 +163,14 @@
             copy.start()
             part_copies.append(copy)
         result[part, :] = mm_t(returned, ip[2 * rim :, :])
-        copy = pltpu.make_async_copy(
-            result.at[part, inner], out_hbm.at[part, inner], store_sem.at[chunk, 0]
-        )
-        copy.start()
-        stores.append(copy)
 
     for chunk in range(CHUNKS):
         part = piece(chunk)
         for side, where, pick, target in ((0, lead, left_pick, right), (1, tail, right_pick, left)):
             pair(part_send, part_recv, part_out, part_in, chunk, side, target).wait_recv()
             result[part, where] += mm_t(part_in[chunk, side], pick)
-            copy = pltpu.make_async_copy(
-                result.at[part, where], out_hbm.at[part, where], store_sem.at[chunk, 1 + side]
-            )
-            copy.start()
-            stores.append(copy)
     for copy in edge_copies + slot_copies + back_copies + part_copies:
         copy.wait_send()
-    for copy in stores:
-        copy.wait()
 
 
 def on_device(tiles, groups, field, interp, conv_blocks, band_shift, owner, edge_index):
@@ -199,30 +184,28 @@
     sides = pltpu.VMEM((CHUNKS, 2, height, rim), half)
     cells = pltpu.VMEM((CHUNKS, groups, height, capacity), half)
     two, many = pltpu.SemaphoreType.DMA((CHUNKS, 2)), pltpu.SemaphoreType.DMA((CHUNKS, groups))
+    lists = jnp.concatenate([owner.reshape(-1), edge_index.reshape(-1), band_shift.reshape(-1)])
+    lists = jnp.pad(lists, (0, -lists.size % 128)).reshape(1, -1)
     anywhere = pl.BlockSpec(memory_space=pl.ANY)
     return pl.pallas_call(
-        functools.partial(kernel, tiles, groups),
+        functools.partial(kernel, tiles, groups, rim),
         out_shape=jax.ShapeDtypeStruct(field.shape, single),
-        in_specs=[anywhere] * 3 + [pl.BlockSpec(memory_space=pltpu.SMEM)] + [anywhere] * 2,
-        out_specs=anywhere,
+        in_specs=[anywhere] * 3 + [pl.BlockSpec(memory_space=pltpu.VMEM)],
+        out_specs=pl.BlockSpec(memory_space=pltpu.VMEM),
         scratch_shapes=[
             pltpu.VMEM(field.shape, single),
             pltpu.VMEM(interp.shape, half),
             pltpu.VMEM(conv_blocks.shape, half),
-            pltpu.VMEM((1, points), jnp.int32),
-            pltpu.VMEM(edge_index.shape, jnp.int32),
             pltpu.VMEM((extended, slots), half),
             pltpu.VMEM((slots, slots), half),
             pltpu.VMEM((slots, slots), half),
             pltpu.VMEM((rows, slots), single),
-            pltpu.VMEM(field.shape, single),
             sides, sides, cells, cells, cells, cells, sides, sides,
             pltpu.SemaphoreType.DMA((7,)),
-            pltpu.SemaphoreType.DMA((CHUNKS, 3)),
             two, two, many, many, many, many, two, two,
         ],
-        compiler_params=pltpu.CompilerParams(collective_id=0, has_side_effects=True),
-    )(field, interp, conv_blocks, band_shift, owner.reshape(1, points), edge_index)
+        compiler_params=pltpu.CompilerParams(collective_id=0, has_side_effects=True, vmem_limit_bytes=53 * 2**20),
+    )(field, interp, conv_blocks, lists)
 
 
 def solution(mesh):

time: 27.1 us -> 26.1 us (0.963)
  Pallas kernels: 24.9 us -> 23.6 us
    pallas_call x1, Pallas kernels: 24.9 us -> 23.6 us  [on_device(): pl.pallas_call(functools.partial(kernel, tiles, groups, rim), out_shape=j...]
    reshape x0 -> x2, local copies, waits for them, and re-layouts: none -> 0.78 us  [the longest x1 0.77 us: on_device(): band_shift.reshape(-1)]
    unnamed x1 -> x5, local copies, waits for them, and re-layouts: 2.06 us -> 1.54 us
where the time goes in v3:
time: 26.1 us; the launch traced here: 25.9 us
  Pallas kernels  23.6 us (90%)
  local copies, waits for them, and re-layouts  2.33 us (9%)
    pallas_call x1, Pallas kernels, on_device(): pl.pallas_call(functools.partial(kernel, tiles, groups, rim), out_shape=j...  23.6 us
    unnamed x5, local copies, waits for them, and re-layouts  1.54 us
    reshape x1, local copies, waits for them, and re-layouts, on_device(): band_shift.reshape(-1)  0.77 us

profile of v3, /device:TPU:0, one launch (start us, length us, event | category | flops | bytes accessed | tf_op | source)
XLA Modules:
  0.0 25.9 jit_solution(1134368827948659442)
XLA Ops:
  0.0 0.0 copy-start
  0.0 0.8 %reshape.14 = s32[6]{0:T(128)S(1)} reshape(s32[2,3]{1,0:T(2,128)} %param.9) | data formatting | bytes 48 | tf_op jit(solution)/shard_map/reshape | solution.py:187
  0.8 0.0 copy-done
  0.8 0.0 copy-start.1
  0.8 0.7 %copy-done.1 = s32[2,128]{1,0:T(2,128)S(1)} copy-done((s32[2,128]{1,0:T(2,128)S(1)}, s32[2,128]{1,0:T(2,128)}, u32[]{:S(2)}) %copy-start.1) | copy-done | bytes 1048
  1.5 23.6 %shard_map.64 = f32[256,768]{1,0:T(8,128)S(1)} custom-call(f32[256,768]{1,0:T(8,128)} %field_hbm.1, bf16[1024,384]{1,0:T(8,128)(2,1)} %interp_hbm.1, bf16[2,3,256,256]{3,2,1,0:T(8,128)(2,1)} %blocks_hbm.1, s32[1,768]{1,0:T(1,128)S(1)} %reshape.15.lists), custom_call_target="tpu_custom_call" | custom-call | tf_op jit(solution)/shard_map/pallas_call | solution.py:190
  25.1 0.9 %copy.8 = f32[256,768]{1,0:T(8,128)} copy(f32[256,768]{1,0:T(8,128)S(1)} %shard_map.64) | data formatting | bytes 1572864
  (4 shorter events, 0.0 us)
Async XLA Ops:
  0.0 0.8 %copy-start = (s32[384,1]{0,1:T(1,128)S(1)}, s32[384,1]{0,1:T(1,128)}, u32[]{:S(2)}) copy-start(s32[384,1]{0,1:T(1,128)} %param.10) | copy-start | bytes 4612
  0.8 0.7 %copy-start.1 = (s32[2,128]{1,0:T(2,128)S(1)}, s32[2,128]{1,0:T(2,128)}, u32[]{:S(2)}) copy-start(s32[2,128]{1,0:T(2,128)} %param.11) | copy-start | bytes 3076
